TPU v7x, 512 devices: a whole 4x8x8 slice. The times are simulated.
512 devices in a mesh: gx: 8 (over x, core), gy: 64 (over y, z).
Axes of the slice: x: 4, y: 8, z: 8, core: 2. Of those that a mesh axis runs over, the one named last changes fastest.
Arguments:
- cell: int32 [16777216], P(('gx', 'gy')), may hold values from 0 to 524287
- vehicle: int32 [16777216], P(('gx', 'gy')), may hold values from 0 to 1023
- speed: float32 [16777216], P(('gx', 'gy')), may hold values from 0 to 64, as said below
Outputs:
- top_speed: float32 [524288], P(('gx', 'gy'))
- top_vehicle: int32 [524288], P(('gx', 'gy'))
Inputs may be any that keep to these rules, and one draw needn't show every extreme that they name: Every speed is a whole multiple of 1/1024.
All inputs are finite; a program needn't handle non-finite values.
Results may differ from a plain program's by a relative error of at most 0.0003.
Values sent between devices are 32-bit elements; how exact they have to be, the bound alone decides.
A program may use at most 64 MiB of HBM per device.

v0:
```python
import jax
import jax.numpy as jnp
import numpy as np
from jax import lax
from jax.experimental import pallas as pl
from jax.experimental.pallas import tpu as pltpu
from jax.sharding import PartitionSpec as P

CELLS = 524288
VEHICLES = 1024
MESH = pl.DeviceIdType.MESH
SIGN = np.int32(-(2**31))
CAP = 2048
EMPTY = 131072


def swapped(block, axis, apart):
    count = lax.axis_size(axis)
    route = []
    for low in range(count):
        high = low | 1 << apart
        if high != low and high < count:
            route += [(low, high), (high, low)]
    return lax.ppermute(block, axis, route)


def combine(first, second):
    speed_a = first[0]
    speed_b = second[0]
    best = jnp.maximum(speed_a, speed_b)
    ident = jnp.where(
        speed_a > speed_b,
        first[1],
        jnp.where(speed_b > speed_a, second[1], jnp.minimum(first[1], second[1])),
    )
    return jnp.stack([best, ident])


def dense_path(cell, vehicle, speed):
    local_best = jnp.full((CELLS,), -1.0, jnp.float32).at[cell].max(speed)
    chosen = jnp.where(speed == local_best[cell], vehicle, VEHICLES)
    local_ident = jnp.full((CELLS,), VEHICLES, jnp.int32).at[cell].min(chosen)
    paired = jnp.stack([local_best, local_ident.astype(jnp.float32)])
    outer = lax.axis_size("gx")
    inner = lax.axis_size("gy")
    nbits = (outer * inner).bit_length() - 1
    myself = lax.axis_index(("gx", "gy"))
    buffer = paired
    for level in reversed(range(nbits)):
        half = buffer.shape[1] // 2
        side = myself >> level & 1
        keep = lax.dynamic_slice_in_dim(buffer, side * half, half, 1)
        give = lax.dynamic_slice_in_dim(buffer, (1 - side) * half, half, 1)
        partner = swapped(give, ("gx", "gy"), level)
        buffer = combine(keep, partner)
    best = buffer[0]
    lowest = buffer[1].astype(jnp.int32)
    return best, jnp.where(lowest < VEHICLES, lowest, -1)


def lanes():
    return lax.broadcasted_iota(jnp.int32, (8, 128), 1)


def subs():
    return lax.broadcasted_iota(jnp.int32, (8, 128), 0)


def lane_pick(x, index):
    return jnp.take_along_axis(x, index, axis=1)


def sub_pick(x, index):
    return jnp.take_along_axis(x, index, axis=0)


def sub_bit(i):
    return ((subs() >> i) & 1) == 1


def lane_bit(i):
    return ((lanes() >> i) & 1) == 1


def total_of(counts, matrix):
    return jnp.dot(counts, matrix, preferred_element_type=jnp.float32)


def above(c1, k1, c2, k2):
    tie = c1 == c2
    return jnp.where(tie, k1, c1) > jnp.where(tie, k2, c2)


def order_pair(a, b, down):
    swap = above(*a, *b)
    if down is True:
        a, b = b, a
    elif down is not False:
        swap = swap ^ down
    low = tuple(jnp.where(swap, y, x) for x, y in zip(a, b))
    high = tuple(jnp.where(swap, x, y) for x, y in zip(a, b))
    return low, high


def order_v(x, bits, down):
    for b in bits:
        for m in range(len(x)):
            if not m >> b & 1:
                x[m], x[m | 1 << b] = order_pair(x[m], x[m | 1 << b], down(m))


def order_cross(x, pick, index, bit, down):
    other = ~bit
    for m in range(len(x)):
        d = down(m)
        wants = bit if d is False else other if d is True else bit ^ d
        c, k = x[m]
        pc, pk = pick(c, index), pick(k, index)
        swap = above(c, k, pc, pk) ^ wants
        x[m] = jnp.where(swap, pc, c), jnp.where(swap, pk, k)


def order_s(x, bits, down):
    for i in bits:
        order_cross(x, sub_pick, subs() ^ (1 << i), sub_bit(i), down)


def order_l(x, bits, down):
    for i in bits:
        order_cross(x, lane_pick, lanes() ^ (1 << i), lane_bit(i), down)


def move_pair(a, b, bit):
    mask = SIGN | np.int32(1 << bit)
    ma, mb = a[0] & mask, b[0] & mask
    a0, b0 = ma == SIGN, mb == SIGN
    a1, b1 = ma == mask, mb == mask
    low = (jnp.where(b0, b[0], jnp.where(a0, a[0], 0)), jnp.where(b0, b[1], a[1]))
    high = (jnp.where(a1, a[0], jnp.where(b1, b[0], 0)), jnp.where(a1, a[1], b[1]))
    return low, high


def move_v(x, steps):
    for bit, i in steps:
        for m in range(len(x)):
            if not m >> i & 1:
                x[m], x[m | 1 << i] = move_pair(x[m], x[m | 1 << i], 16 + bit)


def move_s(x, steps):
    for bit, i in steps:
        b = 16 + bit
        mask = SIGN | np.int32(1 << b)
        here = SIGN | (((subs() >> i) & 1) << b)
        index = subs() ^ (1 << i)
        for m in range(len(x)):
            w, k = x[m]
            pw, pk = sub_pick(w, index), sub_pick(k, index)
            stay, come = (w & mask) == here, (pw & mask) == here
            x[m] = jnp.where(come, pw, jnp.where(stay, w, 0)), jnp.where(come, pk, k)


def turned(x):
    both = []
    for w in range(2):
        t = jnp.concatenate([p[w] for p in x], axis=0).T
        both.append([t[8 * m : 8 * m + 8] for m in range(16)])
    return list(zip(*both))


def batcher(n):
    pairs = []

    def merge(lo, n, r):
        m = r * 2
        if m < n:
            merge(lo, n, m)
            merge(lo + r, n, m)
            for i in range(lo + r, lo + n - r, m):
                pairs.append((i, i + r))
        else:
            pairs.append((lo, lo + r))

    def sort(lo, n):
        if n > 1:
            m = n // 2
            sort(lo, m)
            sort(lo + m, m)
            merge(lo, n, 1)

    sort(0, n)
    return pairs


def total(x):
    s = jnp.sum(x.astype(jnp.float32), axis=0, keepdims=True)
    s = jnp.sum(s, axis=1, keepdims=True)
    return jnp.broadcast_to(s, (8, 128)).astype(jnp.int32)


def sub_prefix(x):
    before, block = jnp.zeros_like(x), x
    for i in range(3):
        other = sub_pick(block, subs() ^ (1 << i))
        before = before + jnp.where(sub_bit(i), other, 0)
        block = block + other
    return before, block


def lane_prefix(x, order):
    row = lax.broadcasted_iota(jnp.int32, (128, 128), 0)
    column = lax.broadcasted_iota(jnp.int32, (128, 128), 1)
    less = jnp.where(order(row) < order(column), 1.0, 0.0).astype(jnp.float32)
    x = x.astype(jnp.float32)
    return total_of(x, less).astype(jnp.int32), total_of(x, jnp.ones((128, 128), jnp.float32)).astype(jnp.int32)


def load(A, B, at):
    return [(A[at + m], B[at + m]) for m in range(16)]


def save(A, B, at, x):
    for m in range(16):
        A[at + m] = x[m][0]
        B[at + m] = x[m][1]


def sort_events(cell, vehicle, speed, A, B):
    flip = -(subs() & 1)
    for block in (0, 16):
        x = []
        for m in range(16):
            c = cell[block + m]
            c = (
                (c & 0x7F800)
                | ((c & 0x380) << 1)
                | ((c & 0x400) >> 3)
                | ((c & 7) << 4)
                | ((c & 0x78) >> 3)
            )
            k = (speed[block + m] * 1024.0).astype(jnp.int32) * 1024 + (1023 - vehicle[block + m])
            x.append((c ^ flip, k ^ flip))
        for i, j in batcher(16):
            x[i], x[j] = order_pair(x[i], x[j], False)
        x = [(c ^ flip, k ^ flip) for c, k in x]
        for top in (1, 2, 3):
            way = sub_bit(top) if top < 3 else block > 0
            order_s(x, reversed(range(top)), lambda m: way)
            order_v(x, (3, 2, 1, 0), lambda m: way)
        save(A, B, block, x)
    for s in range(8, 16):
        way = lane_bit(s - 8) if s < 15 else False
        if s > 10:
            for block in (0, 16):
                x = turned(load(A, B, block))
                down = lambda m: bool(m >> (s - 11) & 1)
                order_v(x, reversed(range(s - 11)), down)
                order_s(x, (2, 1, 0), down)
                save(A, B, block, turned(x))
        for m in range(16):
            pair = [(A[m], B[m]), (A[m + 16], B[m + 16])]
            if s in (9, 10):
                order_l(pair, reversed(range(s - 8)), lambda m: way)
            order_v(pair, (0,), lambda m: way)
            for h in range(2):
                A[m + 16 * h] = pair[h][0]
                B[m + 16 * h] = pair[h][1]
        for block in (0, 16):
            x = load(A, B, block)
            order_s(x, (2, 1, 0), lambda m: way)
            order_v(x, (3, 2, 1, 0), lambda m: way)
            save(A, B, block, x)


def compact_events(A, B):
    lane, sub = lanes(), subs()
    heads = [pltpu.roll(A[block], 7, 0) for block in (0, 16)]
    follows = [
        jnp.where(sub == 7, heads[1], heads[0]),
        jnp.where(sub == 7, pltpu.roll(heads[0], 127, 1), heads[1]),
    ]
    sums = []
    for block in (0, 16):
        run = jnp.zeros((8, 128), jnp.int32)
        for m in range(16):
            c = A[block + m]
            keep = c != (A[block + m + 1] if m < 15 else follows[block // 16])
            if block + m == 31:
                keep = keep | ((sub == 7) & (lane == 127))
            w = (run << 16) | (c & 0xFFFF)
            B[block + m] = B[block + m] | ((c >> 16) << 27)
            A[block + m] = jnp.where(keep, SIGN | w, 0)
            run = run + keep.astype(jnp.int32)
        sums.append(sub_prefix(run))
    ahead, every = lane_prefix(sums[0][1] + sums[1][1], lambda l: l)
    starts = [(ahead + sums[0][0]) << 16, (ahead + sums[0][1] + sums[1][0]) << 16]
    for h in range(2):
        x = load(A, B, 16 * h)
        x = [(jnp.where(w < 0, w + starts[h], 0), k) for w, k in x]
        move_v(x, [(i, i) for i in range(4)])
        move_s(x, [(4 + i, i) for i in range(3)])
        save(A, B, 16 * h, x)
    for m in range(16):
        pair = move_pair((A[m], B[m]), (A[m + 16], B[m + 16]), 16 + 7)
        for h in range(2):
            A[m + 16 * h] = pair[h][0]
            B[m + 16 * h] = pair[h][1]
    y = []
    for h in range(2):
        x = turned(load(A, B, 16 * h))
        move_s(x, [(8 + i, i) for i in range(3)])
        move_v(x, [(11 + i, i) for i in range(4)])
        y += x[:8]
    starts = group_starts([k >> 27 for _, k in y], [w < 0 for w, _ in y])
    flag = crowded(starts) | (every > 8 * CAP).astype(jnp.int32)
    y = aimed([(w, k & 0x7FFFFFF) for w, k in y], [k >> 27 for _, k in y], [w < 0 for w, _ in y], starts, 0xFFFF)
    return y, flag


def list_rank(v):
    lane = lanes()
    return (v & 7) * CAP + (subs() << 8) + ((v >> 3) << 7) + ((lane & 7) << 4) + (lane >> 3)


def group_starts(groups, valid):
    groups = [jnp.where(u, g, 8) for g, u in zip(groups, valid)]
    starts = [jnp.zeros((8, 128), jnp.int32)]
    for j in range(1, 9):
        t = jnp.zeros((8, 128), jnp.int32)
        for g in groups:
            t = t + jnp.where(g < j, 1, 0)
        starts.append(total(t))
    return starts


def crowded(starts):
    most = jnp.zeros((8, 128), jnp.int32)
    for j in range(8):
        most = jnp.maximum(most, starts[j + 1] - starts[j])
    return (most > CAP).astype(jnp.int32)


def aimed(x, groups, valid, starts, mask):
    made = []
    for v, (w, k) in enumerate(x):
        target = list_rank(v)
        moved = jnp.zeros((8, 128), jnp.int32)
        for j in range(1, 8):
            moved = jnp.where(groups[v] == j, j * CAP - starts[j], moved)
        made.append((jnp.where(valid[v], SIGN | ((target + moved) << 16) | (w & mask), 0), k))
    return made


def expand_lists(x):
    move_v(x, [(13, 2), (12, 1), (11, 0)])
    move_s(x, [(10, 2), (9, 1), (8, 0)])
    move_v(x, [(7, 3)])
    x = turned(x)
    move_s(x, [(6, 2), (5, 1), (4, 0)])
    move_v(x, [(3, 3), (2, 2), (1, 1), (0, 0)])
    return turned(x)


def pack_messages(x, out):
    for v, (w, k) in enumerate(x):
        g, h = v & 7, v >> 3
        out[g, h] = jnp.where(w < 0, w & 0xFFFF, EMPTY).astype(jnp.float32)
        out[g, 2 + h] = (k >> 10).astype(jnp.float32) * (1.0 / 1024.0)
        out[g, 4 + h] = (1023 - (k & 1023)).astype(jnp.float32)


def key_of(speed, vehicle):
    return (speed * 1024.0).astype(jnp.int32) * 1024 + (1023 - vehicle.astype(jnp.int32))


def merge_lists(inbox):
    around, back = 7 - subs(), 127 - lanes()
    x = [None] * 16
    for s in range(8):
        for h in range(2):
            pair = (inbox[s, h].astype(jnp.int32), key_of(inbox[s, 2 + h], inbox[s, 4 + h]))
            if s & 1:
                x[8 * (1 - h) + s] = tuple(lane_pick(sub_pick(w, around), back) for w in pair)
            else:
                x[8 * h + s] = pair
    for level in (1, 2, 3):
        down = (lambda m: bool(m >> level & 1)) if level < 3 else (lambda m: False)
        way = lane_bit(3 + level) if level < 3 else False
        order_v(x, reversed(range(level)), down)
        order_s(x, (2, 1, 0), down)
        order_v(x, (3,), down)
        x = turned(x)
        order_s(x, (2, 1, 0), lambda m: way)
        order_v(x, (3, 2, 1, 0), lambda m: way)
        if level < 3:
            x = turned(x)
    return x


def best_of_cells(x):
    lane, sub = lanes(), subs()
    head = pltpu.roll(x[0][0], 7, 0)
    carried = jnp.where(lane < 64, pltpu.roll(head, 64, 1), pltpu.roll(head, 63, 1))
    follow = jnp.where(sub == 7, carried, head)
    run = jnp.zeros((8, 128), jnp.int32)
    y = []
    for m in range(16):
        c, k = x[m]
        keep = c != (x[m + 1][0] if m < 15 else follow)
        if m == 15:
            keep = keep | ((sub == 7) & (lane == 127))
        keep = keep & (c < EMPTY)
        y.append((jnp.where(keep, SIGN | (run << 16) | c, 0), k))
        run = run + keep.astype(jnp.int32)
    within, block = sub_prefix(run)
    ahead, _ = lane_prefix(block, lambda l: (l & 63) * 2 + (l >> 6))
    start = (within + ahead) << 16
    y = [(jnp.where(w < 0, w + start, 0), k) for w, k in y]
    move_v(y, [(i, i) for i in range(4)])
    move_s(y, [(4 + i, i) for i in range(3)])
    y = turned(y)
    move_v(y, [(7, 3)])
    move_s(y, [(8 + i, i) for i in range(3)])
    move_v(y, [(11 + i, i) for i in range(3)])
    return y


def regroup(x):
    y = best_of_cells(x)
    groups = [(w >> 13) & 7 for w, _ in y]
    valid = [w < 0 for w, _ in y]
    starts = group_starts(groups, valid)
    return expand_lists(aimed(y, groups, valid, starts, 0x1FFF)), crowded(starts)


def to_table(x):
    y = best_of_cells(x)
    z = []
    for q in range(4):
        for h in range(2):
            w, k = y[8 * h + q]
            z.append((jnp.where(w < 0, SIGN | ((w & 0x1FFF) << 16), 0), k))
    move_v(z, [(12, 2), (11, 1)])
    move_s(z, [(10, 2), (9, 1), (8, 0)])
    move_v(z, [(7, 0)])
    none = jnp.zeros((8, 128), jnp.int32)
    z = turned(z + [(none, none)] * 8)
    move_s(z, [(6, 2), (5, 1), (4, 0)])
    move_v(z, [(3, 3), (2, 2), (1, 1), (0, 0)])
    return turned(z)[:8]


def exchange_kernel(cell, vehicle, speed, best, ident, flags, A, B, out1, in1, out2, in2, out3, in3, mark, marks1, mark2,
                    marks2, send, recv):
    gx, gy = lax.axis_index("gx"), lax.axis_index("gy")
    y, z = gy // 8, gy % 8

    def peer(phase, j):
        if phase == 0:
            return (gx ^ j, gy)
        if phase == 1:
            return (gx, (y ^ j) * 8 + z)
        return (gx, y * 8 + (z ^ j))

    barrier = pltpu.get_barrier_semaphore()
    for phase in range(3):
        for j in range(1, 8):
            pl.semaphore_signal(barrier, inc=1, device_id=peer(phase, j), device_id_type=MESH)

    def copies(row, phase, source, target):
        return [
            pltpu.make_async_remote_copy(
                src_ref=source(j),
                dst_ref=target.at[j],
                send_sem=send.at[row, j],
                recv_sem=recv.at[row, j],
                device_id=peer(phase, j),
                device_id_type=MESH,
            )
            for j in range(1, 8)
        ]

    sort_events(cell, vehicle, speed, A, B)
    x, flag = compact_events(A, B)
    pack_messages(expand_lists(x), out1)
    pl.semaphore_wait(barrier, 21)
    first = copies(0, 0, lambda j: out1.at[gx ^ j], in1)
    for c in first:
        c.start()
    in1[0] = out1[gx]
    for c in first:
        c.wait_recv()

    x, more = regroup(merge_lists(in1))
    mark[...] = (flag | more).astype(jnp.float32)
    pack_messages(x, out2)
    second = copies(1, 1, lambda j: out2.at[y ^ j], in2)
    for c in second:
        c.start()
    flags1 = copies(2, 0, lambda j: mark, marks1)
    for c in flags1:
        c.start()
    in2[0] = out2[y]
    for c in flags1:
        c.wait_recv()
    seen = mark[...]
    for j in range(1, 8):
        seen = jnp.maximum(seen, marks1[j])
    mark2[...] = seen
    flags2 = copies(3, 1, lambda j: mark2, marks2)
    for c in flags2:
        c.start()
    for c in second:
        c.wait_recv()

    table = to_table(merge_lists(in2))
    for c in flags2:
        c.wait_recv()
    for j in range(1, 8):
        seen = jnp.maximum(seen, marks2[j])
    for v, (w, k) in enumerate(table):
        there = w < 0
        out3[v, 0] = jnp.where(there, (k >> 10).astype(jnp.float32) * (1.0 / 1024.0), -1.0)
        out3[v, 1] = jnp.where(there, (1023 - (k & 1023)).astype(jnp.float32), 1024.0) + seen * 4096.0
    third = copies(4, 2, lambda j: out3.at[z ^ j], in3)
    for c in third:
        c.start()
    in3[0] = out3[z]
    for c in third:
        c.wait_recv()
    k = key_of(in3[0, 0], in3[0, 1])
    most = in3[0, 1]
    for j in range(1, 8):
        k = jnp.maximum(k, key_of(in3[j, 0], in3[j, 1]))
        most = jnp.maximum(most, in3[j, 1])
    best[...] = jnp.where(k < 0, -1.0, (k >> 10).astype(jnp.float32) * (1.0 / 1024.0))
    ident[...] = jnp.where(k < 0, -1, 1023 - (k & 1023))
    flags[0, 0] = jnp.max(most).astype(jnp.int32)
    for group in (first, second, flags1, flags2, third):
        for c in group:
            c.wait_send()


def words(*shape):
    return pltpu.VMEM(shape + (8, 128), jnp.float32)


def sparse_path(cell, vehicle, speed):
    whole = pl.BlockSpec(memory_space=pltpu.VMEM)
    ints = lambda n: pltpu.VMEM((n, 8, 128), jnp.int32)
    return pl.pallas_call(
        exchange_kernel,
        out_shape=(
            jax.ShapeDtypeStruct((8, 128), jnp.float32),
            jax.ShapeDtypeStruct((8, 128), jnp.int32),
            jax.ShapeDtypeStruct((1, 1), jnp.int32),
        ),
        in_specs=[whole] * 3,
        out_specs=(whole, whole, pl.BlockSpec(memory_space=pltpu.SMEM)),
        scratch_shapes=[
            ints(32), ints(32),
            words(8, 6), words(8, 6), words(8, 6), words(8, 6), words(8, 2), words(8, 2),
            words(), words(8), words(), words(8),
            pltpu.SemaphoreType.DMA((5, 8)),
            pltpu.SemaphoreType.DMA((5, 8)),
        ],
        compiler_params=pltpu.CompilerParams(collective_id=0, has_side_effects=True),
    )(cell, vehicle, speed)


def per_device(cell, vehicle, speed):
    shaped = [x.reshape(32, 8, 128) for x in (cell, vehicle, speed)]
    best, ident, flags = sparse_path(*shaped)
    return lax.cond(
        flags[0, 0] > 2048,
        lambda: dense_path(cell, vehicle, speed),
        lambda: (best.reshape(1024), ident.reshape(1024)),
    )


def solution(mesh):
    placed = (P(("gx", "gy")), P(("gx", "gy")), P(("gx", "gy")))
    return jax.shard_map(
        per_device,
        mesh=mesh,
        in_specs=placed,
        out_specs=(P(("gx", "gy")), P(("gx", "gy"))),
        check_vma=False,
    )
```

profile of v0, /device:TPU:1, one launch (start us, length us, event | category | flops | bytes accessed | tf_op | source)
XLA Modules:
  0.0 43.0 jit_solution(8639390224824976930)
XLA Ops:
  0.6 40.3 %shard_map.54 = (f32[8,128]{1,0:T(8,128)S(1)}, s32[8,128]{1,0:T(8,128)S(1)}, s32[1,1]{1,0:T(1,128)}) custom-call(s32[32,8,128]{2,1,0:T(8,128)} %bitcast.13, s32[32,8,128]{2,1,0:T(8,128)} %bitcast.14, f32[32,8,128]{2,1,0:T(8,128)} %bitcast.15), custom_call_target="tpu_custom_call" | custom-call | tf_op jit(solution)/shard_map/pallas_call | solution.py:551
  41.6 0.2 conditional.1
  41.8 0.6 %copy.15 = f32[1024]{0:T(1024)} copy(f32[1024]{0:T(1024)S(1)} %get-tuple-element.72) | data formatting | bytes 8192
  42.4 0.6 %copy.16 = s32[1024]{0:T(1024)} copy(s32[1024]{0:T(1024)S(1)} %get-tuple-element.73) | data formatting | bytes 8192
where the time goes:
time: 43.1 us; the launch traced here: 43 us
  Pallas kernels  40.3 us (94%)
  between operations  1.27 us (3%)
  local copies, waits for them, and re-layouts  1.19 us (3%)
    pallas_call x1, Pallas kernels, sparse_path(): pl.pallas_call(exchange_kernel, out_shape=(jax.ShapeDtypeStruct((8, 128),...  40.3 us
    unnamed x2, local copies, waits for them, and re-layouts  1.19 us

commit v1 on v0

--- a/solution.py
+++ b/solution.py
@@ -11,6 +11,7 @@
 MESH = pl.DeviceIdType.MESH
 SIGN = np.int32(-(2**31))
 CAP = 2048
+SHORT = 1536
 EMPTY = 131072
 
 
@@ -55,7 +56,8 @@
         buffer = combine(keep, partner)
     best = buffer[0]
     lowest = buffer[1].astype(jnp.int32)
-    return best, jnp.where(lowest < VEHICLES, lowest, -1)
+    top_vehicle = jnp.where(lowest < VEHICLES, lowest, -1)
+    return jnp.stack([best, top_vehicle.astype(jnp.float32)]).reshape(2, 8, 128)
 
 
 def lanes():
@@ -207,12 +209,12 @@
     return before, block
 
 
-def lane_prefix(x, order):
+def lane_prefix(x, order, places):
     row = lax.broadcasted_iota(jnp.int32, (128, 128), 0)
     column = lax.broadcasted_iota(jnp.int32, (128, 128), 1)
-    less = jnp.where(order(row) < order(column), 1.0, 0.0).astype(jnp.float32)
     x = x.astype(jnp.float32)
-    return total_of(x, less).astype(jnp.int32), total_of(x, jnp.ones((128, 128), jnp.float32)).astype(jnp.int32)
+    before = [jnp.where(order(row) < place(column), 1.0, 0.0).astype(jnp.float32) for place in places]
+    return [total_of(x, m).astype(jnp.int32) for m in before + [jnp.ones((128, 128), jnp.float32)]]
 
 
 def load(A, B, at):
@@ -231,42 +233,38 @@
         x = []
         for m in range(16):
             c = cell[block + m]
-            c = (
-                (c & 0x7F800)
-                | ((c & 0x380) << 1)
-                | ((c & 0x400) >> 3)
-                | ((c & 7) << 4)
-                | ((c & 0x78) >> 3)
-            )
+            c = (c & 0x7FF80) | ((c & 7) << 4) | ((c >> 3) & 15)
             k = (speed[block + m] * 1024.0).astype(jnp.int32) * 1024 + (1023 - vehicle[block + m])
             x.append((c ^ flip, k ^ flip))
         for i, j in batcher(16):
             x[i], x[j] = order_pair(x[i], x[j], False)
         x = [(c ^ flip, k ^ flip) for c, k in x]
         for top in (1, 2, 3):
-            way = sub_bit(top) if top < 3 else block > 0
+            way = sub_bit(top) if top < 3 else lane_bit(0)
             order_s(x, reversed(range(top)), lambda m: way)
             order_v(x, (3, 2, 1, 0), lambda m: way)
         save(A, B, block, x)
     for s in range(8, 16):
-        way = lane_bit(s - 8) if s < 15 else False
         if s > 10:
             for block in (0, 16):
                 x = turned(load(A, B, block))
-                down = lambda m: bool(m >> (s - 11) & 1)
-                order_v(x, reversed(range(s - 11)), down)
-                order_s(x, (2, 1, 0), down)
-                save(A, B, block, turned(x))
-        for m in range(16):
-            pair = [(A[m], B[m]), (A[m + 16], B[m + 16])]
-            if s in (9, 10):
-                order_l(pair, reversed(range(s - 8)), lambda m: way)
-            order_v(pair, (0,), lambda m: way)
-            for h in range(2):
-                A[m + 16 * h] = pair[h][0]
-                B[m + 16 * h] = pair[h][1]
+                order_v(x, reversed(range(s - 11)), lambda m: bool(m >> (s - 11) & 1))
+                save(A, B, block, x)
+            for m in range(16):
+                pair = [(A[m], B[m]), (A[m + 16], B[m + 16])]
+                order_v(pair, (0,), lambda _: bool(m >> (s - 11) & 1))
+                for h in range(2):
+                    A[m + 16 * h] = pair[h][0]
+                    B[m + 16 * h] = pair[h][1]
         for block in (0, 16):
             x = load(A, B, block)
+            way = lane_bit(s - 7) if s < 10 else block > 0 if s == 10 else lane_bit(s - 8) if s < 15 else False
+            if s > 9:
+                x = turned(x) if s == 10 else x
+                order_s(x, (2, 1, 0), lambda m: way if s == 10 else bool(m >> (s - 11) & 1))
+                x = turned(x)
+            else:
+                order_l(x, reversed(range(s - 7)), lambda m: way)
             order_s(x, (2, 1, 0), lambda m: way)
             order_v(x, (3, 2, 1, 0), lambda m: way)
             save(A, B, block, x)
@@ -275,9 +273,11 @@
 def compact_events(A, B):
     lane, sub = lanes(), subs()
     heads = [pltpu.roll(A[block], 7, 0) for block in (0, 16)]
+    nexts = [pltpu.roll(x, 127, 1) for x in heads]
+    edge = (lane & 7) == 7
     follows = [
-        jnp.where(sub == 7, heads[1], heads[0]),
-        jnp.where(sub == 7, pltpu.roll(heads[0], 127, 1), heads[1]),
+        jnp.where(sub == 7, jnp.where(edge, pltpu.roll(heads[1], 7, 1), nexts[0]), heads[0]),
+        jnp.where(sub == 7, jnp.where(edge, nexts[0], nexts[1]), heads[1]),
     ]
     sums = []
     for block in (0, 16):
@@ -292,34 +292,36 @@
             A[block + m] = jnp.where(keep, SIGN | w, 0)
             run = run + keep.astype(jnp.int32)
         sums.append(sub_prefix(run))
-    ahead, every = lane_prefix(sums[0][1] + sums[1][1], lambda l: l)
-    starts = [(ahead + sums[0][0]) << 16, (ahead + sums[0][1] + sums[1][0]) << 16]
+    orders = [lambda l: ((l >> 3) << 4) + (l & 7), lambda l: ((l >> 3) << 4) + (l & 7) + 8]
+    parts = [lane_prefix(sums[h][1], orders[h], orders) for h in range(2)]
+    every = parts[0][2] + parts[1][2]
     for h in range(2):
-        x = load(A, B, 16 * h)
-        x = [(jnp.where(w < 0, w + starts[h], 0), k) for w, k in x]
+        start = (parts[0][h] + parts[1][h] + sums[h][0]) << 16
+        x = [(jnp.where(w < 0, w + start, 0), k) for w, k in load(A, B, 16 * h)]
         move_v(x, [(i, i) for i in range(4)])
         move_s(x, [(4 + i, i) for i in range(3)])
+        x = turned(x)
+        move_s(x, [(7 + i, i) for i in range(3)])
         save(A, B, 16 * h, x)
     for m in range(16):
-        pair = move_pair((A[m], B[m]), (A[m + 16], B[m + 16]), 16 + 7)
+        pair = move_pair((A[m], B[m]), (A[m + 16], B[m + 16]), 16 + 10)
         for h in range(2):
             A[m + 16 * h] = pair[h][0]
             B[m + 16 * h] = pair[h][1]
     y = []
     for h in range(2):
-        x = turned(load(A, B, 16 * h))
-        move_s(x, [(8 + i, i) for i in range(3)])
+        x = load(A, B, 16 * h)
         move_v(x, [(11 + i, i) for i in range(4)])
         y += x[:8]
     starts = group_starts([k >> 27 for _, k in y], [w < 0 for w, _ in y])
-    flag = crowded(starts) | (every > 8 * CAP).astype(jnp.int32)
+    flag = crowded(starts, CAP) | (every > 8 * CAP).astype(jnp.int32)
     y = aimed([(w, k & 0x7FFFFFF) for w, k in y], [k >> 27 for _, k in y], [w < 0 for w, _ in y], starts, 0xFFFF)
     return y, flag
 
 
 def list_rank(v):
     lane = lanes()
-    return (v & 7) * CAP + (subs() << 8) + ((v >> 3) << 7) + ((lane & 7) << 4) + (lane >> 3)
+    return (v & 7) * CAP + ((v >> 3) << 10) + (subs() << 7) + ((lane & 7) << 4) + (lane >> 3)
 
 
 def group_starts(groups, valid):
@@ -333,11 +335,11 @@
     return starts
 
 
-def crowded(starts):
+def crowded(starts, room):
     most = jnp.zeros((8, 128), jnp.int32)
     for j in range(8):
         most = jnp.maximum(most, starts[j + 1] - starts[j])
-    return (most > CAP).astype(jnp.int32)
+    return (most > room).astype(jnp.int32)
 
 
 def aimed(x, groups, valid, starts, mask):
@@ -352,21 +354,36 @@
 
 
 def expand_lists(x):
-    move_v(x, [(13, 2), (12, 1), (11, 0)])
-    move_s(x, [(10, 2), (9, 1), (8, 0)])
-    move_v(x, [(7, 3)])
+    move_v(x, [(13, 2), (12, 1), (11, 0), (10, 3)])
+    move_s(x, [(9, 2), (8, 1), (7, 0)])
     x = turned(x)
     move_s(x, [(6, 2), (5, 1), (4, 0)])
     move_v(x, [(3, 3), (2, 2), (1, 1), (0, 0)])
     return turned(x)
 
 
+def planes(w, k):
+    return (
+        jnp.where(w < 0, w & 0xFFFF, EMPTY).astype(jnp.float32),
+        (k >> 10).astype(jnp.float32) * (1.0 / 1024.0),
+        (1023 - (k & 1023)).astype(jnp.float32),
+    )
+
+
 def pack_messages(x, out):
-    for v, (w, k) in enumerate(x):
-        g, h = v & 7, v >> 3
-        out[g, h] = jnp.where(w < 0, w & 0xFFFF, EMPTY).astype(jnp.float32)
-        out[g, 2 + h] = (k >> 10).astype(jnp.float32) * (1.0 / 1024.0)
-        out[g, 4 + h] = (1023 - (k & 1023)).astype(jnp.float32)
+    for v, pair in enumerate(x):
+        for p, plane in enumerate(planes(*pair)):
+            out[v & 7, 2 * p + (v >> 3)] = plane
+
+
+def pack_short(x, out):
+    for v, pair in enumerate(x):
+        for p, plane in enumerate(planes(*pair)):
+            if v < 8:
+                out[v, 3 * p] = plane[:4]
+                out[v, 3 * p + 1] = plane[4:]
+            else:
+                out[v - 8, 3 * p + 2] = plane[:4]
 
 
 def key_of(speed, vehicle):
@@ -386,9 +403,8 @@
     for level in (1, 2, 3):
         down = (lambda m: bool(m >> level & 1)) if level < 3 else (lambda m: False)
         way = lane_bit(3 + level) if level < 3 else False
-        order_v(x, reversed(range(level)), down)
+        order_v(x, (*reversed(range(level)), 3), down)
         order_s(x, (2, 1, 0), down)
-        order_v(x, (3,), down)
         x = turned(x)
         order_s(x, (2, 1, 0), lambda m: way)
         order_v(x, (3, 2, 1, 0), lambda m: way)
@@ -400,7 +416,8 @@
 def best_of_cells(x):
     lane, sub = lanes(), subs()
     head = pltpu.roll(x[0][0], 7, 0)
-    carried = jnp.where(lane < 64, pltpu.roll(head, 64, 1), pltpu.roll(head, 63, 1))
+    beyond = jnp.where(lane < 64, pltpu.roll(head, 71, 1), pltpu.roll(head, 63, 1))
+    carried = jnp.where((lane & 7) == 7, beyond, pltpu.roll(head, 127, 1))
     follow = jnp.where(sub == 7, carried, head)
     run = jnp.zeros((8, 128), jnp.int32)
     y = []
@@ -413,15 +430,15 @@
         y.append((jnp.where(keep, SIGN | (run << 16) | c, 0), k))
         run = run + keep.astype(jnp.int32)
     within, block = sub_prefix(run)
-    ahead, _ = lane_prefix(block, lambda l: (l & 63) * 2 + (l >> 6))
+    order = lambda l: (((l >> 3) & 7) << 4) + ((l >> 6) << 3) + (l & 7)
+    ahead = lane_prefix(block, order, [order])[0]
     start = (within + ahead) << 16
     y = [(jnp.where(w < 0, w + start, 0), k) for w, k in y]
     move_v(y, [(i, i) for i in range(4)])
     move_s(y, [(4 + i, i) for i in range(3)])
     y = turned(y)
-    move_v(y, [(7, 3)])
-    move_s(y, [(8 + i, i) for i in range(3)])
-    move_v(y, [(11 + i, i) for i in range(3)])
+    move_s(y, [(7 + i, i) for i in range(3)])
+    move_v(y, [(10, 3), (11, 0), (12, 1), (13, 2)])
     return y
 
 
@@ -430,27 +447,49 @@
     groups = [(w >> 13) & 7 for w, _ in y]
     valid = [w < 0 for w, _ in y]
     starts = group_starts(groups, valid)
-    return expand_lists(aimed(y, groups, valid, starts, 0x1FFF)), crowded(starts)
-
-
-def to_table(x):
-    y = best_of_cells(x)
-    z = []
-    for q in range(4):
-        for h in range(2):
-            w, k = y[8 * h + q]
-            z.append((jnp.where(w < 0, SIGN | ((w & 0x1FFF) << 16), 0), k))
-    move_v(z, [(12, 2), (11, 1)])
-    move_s(z, [(10, 2), (9, 1), (8, 0)])
-    move_v(z, [(7, 0)])
-    none = jnp.zeros((8, 128), jnp.int32)
-    z = turned(z + [(none, none)] * 8)
-    move_s(z, [(6, 2), (5, 1), (4, 0)])
-    move_v(z, [(3, 3), (2, 2), (1, 1), (0, 0)])
-    return turned(z)[:8]
-
-
-def exchange_kernel(cell, vehicle, speed, best, ident, flags, A, B, out1, in1, out2, in2, out3, in3, mark, marks1, mark2,
+    return expand_lists(aimed(y, groups, valid, starts, 0x1FFF)), crowded(starts, SHORT)
+
+
+def short_list(inbox, s):
+    made = []
+    for h in range(2):
+        low, high = (3 * h, 1) if h == 0 else (2, 2)
+        c, speed, vehicle = (
+            jnp.concatenate([inbox[s, 3 * p + low], inbox[s, 3 * p + high]], axis=0) for p in range(3)
+        )
+        used = c < EMPTY
+        if h:
+            used = used & (subs() < 4)
+        made.append((jnp.where(used, SIGN | (c.astype(jnp.int32) << 16), 0), key_of(speed, vehicle)))
+    return made
+
+
+def spread_lists(inbox, s):
+    x = []
+    mask = SIGN | np.int32(3 << 27)
+    for t in (s, s + 1):
+        pair = short_list(inbox, t)
+        for high in range(4):
+            mine = SIGN | np.int32(high << 27)
+            some = [(jnp.where((w & mask) == mine, w, 0), k) for w, k in pair]
+            move_v(some, [(10, 0)])
+            x += some
+    move_s(x, [(9, 2), (8, 1), (7, 0)])
+    x = turned(x)
+    move_s(x, [(6, 2), (5, 1), (4, 0)])
+    move_v(x, [(3, 3), (2, 2), (1, 1), (0, 0)])
+    return [jnp.where(w < 0, k, -1) for w, k in x]
+
+
+def joined(tables):
+    best = tables[0]
+    for t in tables[1:]:
+        best = [jnp.maximum(a, b) for a, b in zip(best, t)]
+    t = jnp.concatenate(best, axis=0).T
+    return [jnp.maximum(t[8 * z : 8 * z + 8], t[64 + 8 * z : 72 + 8 * z]) for z in range(8)]
+
+
+def exchange_kernel(cell, vehicle, speed, both, flags, A, B, out1, in1, out2, in2, out3, in3, mark, marks1, mark2,
                     marks2, send, recv):
     gx, gy = lax.axis_index("gx"), lax.axis_index("gy")
     y, z = gy // 8, gy % 8
@@ -493,7 +532,7 @@
 
     x, more = regroup(merge_lists(in1))
     mark[...] = (flag | more).astype(jnp.float32)
-    pack_messages(x, out2)
+    pack_short(x, out2)
     second = copies(1, 1, lambda j: out2.at[y ^ j], in2)
     for c in second:
         c.start()
@@ -510,16 +549,19 @@
     flags2 = copies(3, 1, lambda j: mark2, marks2)
     for c in flags2:
         c.start()
-    for c in second:
-        c.wait_recv()
-
-    table = to_table(merge_lists(in2))
+    tables = []
+    for s in range(0, 8, 2):
+        for j in (s, s + 1):
+            if j:
+                second[j - 1].wait_recv()
+        tables.append(spread_lists(in2, s))
+    table = joined(tables)
     for c in flags2:
         c.wait_recv()
     for j in range(1, 8):
         seen = jnp.maximum(seen, marks2[j])
-    for v, (w, k) in enumerate(table):
-        there = w < 0
+    for v, k in enumerate(table):
+        there = k >= 0
         out3[v, 0] = jnp.where(there, (k >> 10).astype(jnp.float32) * (1.0 / 1024.0), -1.0)
         out3[v, 1] = jnp.where(there, (1023 - (k & 1023)).astype(jnp.float32), 1024.0) + seen * 4096.0
     third = copies(4, 2, lambda j: out3.at[z ^ j], in3)
@@ -533,8 +575,8 @@
     for j in range(1, 8):
         k = jnp.maximum(k, key_of(in3[j, 0], in3[j, 1]))
         most = jnp.maximum(most, in3[j, 1])
-    best[...] = jnp.where(k < 0, -1.0, (k >> 10).astype(jnp.float32) * (1.0 / 1024.0))
-    ident[...] = jnp.where(k < 0, -1, 1023 - (k & 1023))
+    both[0] = jnp.where(k < 0, -1.0, (k >> 10).astype(jnp.float32) * (1.0 / 1024.0))
+    both[1] = jnp.where(k < 0, -1, 1023 - (k & 1023)).astype(jnp.float32)
     flags[0, 0] = jnp.max(most).astype(jnp.int32)
     for group in (first, second, flags1, flags2, third):
         for c in group:
@@ -551,15 +593,14 @@
     return pl.pallas_call(
         exchange_kernel,
         out_shape=(
-            jax.ShapeDtypeStruct((8, 128), jnp.float32),
-            jax.ShapeDtypeStruct((8, 128), jnp.int32),
+            jax.ShapeDtypeStruct((2, 8, 128), jnp.float32),
             jax.ShapeDtypeStruct((1, 1), jnp.int32),
         ),
         in_specs=[whole] * 3,
-        out_specs=(whole, whole, pl.BlockSpec(memory_space=pltpu.SMEM)),
+        out_specs=(whole, pl.BlockSpec(memory_space=pltpu.SMEM)),
         scratch_shapes=[
             ints(32), ints(32),
-            words(8, 6), words(8, 6), words(8, 6), words(8, 6), words(8, 2), words(8, 2),
+            words(8, 6), words(8, 6), pltpu.VMEM((8, 9, 4, 128), jnp.float32), pltpu.VMEM((8, 9, 4, 128), jnp.float32), words(8, 2), words(8, 2),
             words(), words(8), words(), words(8),
             pltpu.SemaphoreType.DMA((5, 8)),
             pltpu.SemaphoreType.DMA((5, 8)),
@@ -570,12 +611,9 @@
 
 def per_device(cell, vehicle, speed):
     shaped = [x.reshape(32, 8, 128) for x in (cell, vehicle, speed)]
-    best, ident, flags = sparse_path(*shaped)
-    return lax.cond(
-        flags[0, 0] > 2048,
-        lambda: dense_path(cell, vehicle, speed),
-        lambda: (best.reshape(1024), ident.reshape(1024)),
-    )
+    both, flags = sparse_path(*shaped)
+    both = lax.cond(flags[0, 0] > 2048, lambda: dense_path(cell, vehicle, speed), lambda: both)
+    return both[0].reshape(1024), both[1].astype(jnp.int32).reshape(1024)
 
 
 def solution(mesh):

time: 43.1 us -> 40.5 us (0.940)
  Pallas kernels: 40.3 us -> 38.2 us
  local copies, waits for them, and re-layouts: 1.19 us -> 0 us
  other arithmetic: 0 us -> 0.6 us
    pallas_call x1, Pallas kernels: 40.3 us -> 38.2 us  [sparse_path(): pl.pallas_call(exchange_kernel, out_shape=(jax.ShapeDtypeStruct((2, 8, 12...]
    unnamed x2 -> x0, local copies, waits for them, and re-layouts: 1.19 us -> none
    convert_element_type x0 -> x1, other arithmetic: none -> 0.6 us  [per_device(): return (both[0].reshape(1024), both[1].astype(jnp.int32).reshape(1024))]
where the time goes in v1:
time: 40.5 us; the launch traced here: 40.4 us
  Pallas kernels  38.2 us (94%)
  between operations  1.32 us (3%)
  other arithmetic  0.6 us (1%)
    pallas_call x1, Pallas kernels, sparse_path(): pl.pallas_call(exchange_kernel, out_shape=(jax.ShapeDtypeStruct((2, 8, 12...  38.2 us

profile of v1, /device:TPU:1, one launch (start us, length us, event | category | flops | bytes accessed | tf_op | source)
XLA Modules:
  0.0 40.4 jit_solution(2607745290215032277)
XLA Ops:
  0.6 38.2 %shard_map.50 = (f32[2,8,128]{2,1,0:T(8,128)S(1)}, s32[1,1]{1,0:T(1,128)}) custom-call(s32[32,8,128]{2,1,0:T(8,128)} %bitcast.14, s32[32,8,128]{2,1,0:T(8,128)} %bitcast.15, f32[32,8,128]{2,1,0:T(8,128)} %bitcast.16), custom_call_target="tpu_custom_call" | custom-call | tf_op jit(solution)/shard_map/pallas_call | solution.py:593
  39.5 0.2 conditional.1
  39.8 0.6 %fusion.23 = (s32[1024]{0:T(1024)}, f32[1024]{0:T(1024)}) fusion(f32[2,8,128]{2,1,0:T(8,128)S(1)} %get-tuple-element.57), kind=kLoop, calls=%fused_computation.95 | loop fusion | flops 1024 | bytes 16384 | tf_op jit(solution)/shard_map/convert_element_type | solution.py:616

commit v2 on v1

--- a/solution.py
+++ b/solution.py
@@ -9,6 +9,7 @@
 CELLS = 524288
 VEHICLES = 1024
 MESH = pl.DeviceIdType.MESH
+FAR_FIRST = ((4, 5, 6, 7, 2, 3, 1), (4, 5, 3, 7, 6, 2, 1), (4, 5, 3, 7, 6, 2, 1))
 SIGN = np.int32(-(2**31))
 CAP = 2048
 SHORT = 1536
@@ -88,13 +89,17 @@
     return jnp.dot(counts, matrix, preferred_element_type=jnp.float32)
 
 
-def above(c1, k1, c2, k2):
-    tie = c1 == c2
-    return jnp.where(tie, k1, c1) > jnp.where(tie, k2, c2)
-
-
-def order_pair(a, b, down):
-    swap = above(*a, *b)
+def above(x, y):
+    tie = x[0] == y[0]
+    return jnp.where(tie, x[1], x[0]) > jnp.where(tie, y[1], y[0])
+
+
+def over(x, y):
+    return x[0] > y[0]
+
+
+def order_pair(a, b, down, more=above):
+    swap = more(a, b)
     if down is True:
         a, b = b, a
     elif down is not False:
@@ -104,32 +109,36 @@
     return low, high
 
 
-def order_v(x, bits, down):
+def order_v(x, bits, down, more=above):
     for b in bits:
         for m in range(len(x)):
             if not m >> b & 1:
-                x[m], x[m | 1 << b] = order_pair(x[m], x[m | 1 << b], down(m))
-
-
-def order_cross(x, pick, index, bit, down):
+                x[m], x[m | 1 << b] = order_pair(x[m], x[m | 1 << b], down(m), more)
+
+
+def order_cross(x, pick, index, bit, down, more):
     other = ~bit
     for m in range(len(x)):
         d = down(m)
         wants = bit if d is False else other if d is True else bit ^ d
         c, k = x[m]
         pc, pk = pick(c, index), pick(k, index)
-        swap = above(c, k, pc, pk) ^ wants
+        if more is above:
+            swap = above((c, k), (pc, pk)) ^ wants
+        else:
+            turn = jnp.where(wants, -1, 0)
+            swap = (c ^ turn) > (pc ^ turn)
         x[m] = jnp.where(swap, pc, c), jnp.where(swap, pk, k)
 
 
-def order_s(x, bits, down):
+def order_s(x, bits, down, more=above):
     for i in bits:
-        order_cross(x, sub_pick, subs() ^ (1 << i), sub_bit(i), down)
-
-
-def order_l(x, bits, down):
+        order_cross(x, sub_pick, subs() ^ (1 << i), sub_bit(i), down, more)
+
+
+def order_l(x, bits, down, more=above):
     for i in bits:
-        order_cross(x, lane_pick, lanes() ^ (1 << i), lane_bit(i), down)
+        order_cross(x, lane_pick, lanes() ^ (1 << i), lane_bit(i), down, more)
 
 
 def move_pair(a, b, bit):
@@ -234,25 +243,26 @@
         for m in range(16):
             c = cell[block + m]
             c = (c & 0x7FF80) | ((c & 7) << 4) | ((c >> 3) & 15)
-            k = (speed[block + m] * 1024.0).astype(jnp.int32) * 1024 + (1023 - vehicle[block + m])
-            x.append((c ^ flip, k ^ flip))
+            level = (speed[block + m] * 1024.0).astype(jnp.int32)
+            w = ((c << 13) | (level >> 4)) ^ SIGN
+            x.append((w ^ flip, ((level & 15) << 10) | (1023 - vehicle[block + m])))
         for i, j in batcher(16):
-            x[i], x[j] = order_pair(x[i], x[j], False)
-        x = [(c ^ flip, k ^ flip) for c, k in x]
+            x[i], x[j] = order_pair(x[i], x[j], False, over)
+        x = [(w ^ flip, k) for w, k in x]
         for top in (1, 2, 3):
             way = sub_bit(top) if top < 3 else lane_bit(0)
-            order_s(x, reversed(range(top)), lambda m: way)
-            order_v(x, (3, 2, 1, 0), lambda m: way)
+            order_s(x, reversed(range(top)), lambda m: way, over)
+            order_v(x, (3, 2, 1, 0), lambda m: way, over)
         save(A, B, block, x)
     for s in range(8, 16):
         if s > 10:
             for block in (0, 16):
                 x = turned(load(A, B, block))
-                order_v(x, reversed(range(s - 11)), lambda m: bool(m >> (s - 11) & 1))
+                order_v(x, reversed(range(s - 11)), lambda m: bool(m >> (s - 11) & 1), over)
                 save(A, B, block, x)
             for m in range(16):
                 pair = [(A[m], B[m]), (A[m + 16], B[m + 16])]
-                order_v(pair, (0,), lambda _: bool(m >> (s - 11) & 1))
+                order_v(pair, (0,), lambda _: bool(m >> (s - 11) & 1), over)
                 for h in range(2):
                     A[m + 16 * h] = pair[h][0]
                     B[m + 16 * h] = pair[h][1]
@@ -261,18 +271,41 @@
             way = lane_bit(s - 7) if s < 10 else block > 0 if s == 10 else lane_bit(s - 8) if s < 15 else False
             if s > 9:
                 x = turned(x) if s == 10 else x
-                order_s(x, (2, 1, 0), lambda m: way if s == 10 else bool(m >> (s - 11) & 1))
+                order_s(x, (2, 1, 0), lambda m: way if s == 10 else bool(m >> (s - 11) & 1), over)
                 x = turned(x)
             else:
-                order_l(x, reversed(range(s - 7)), lambda m: way)
-            order_s(x, (2, 1, 0), lambda m: way)
-            order_v(x, (3, 2, 1, 0), lambda m: way)
+                order_l(x, reversed(range(s - 7)), lambda m: way, over)
+            order_s(x, (2, 1, 0), lambda m: way, over)
+            order_v(x, (3, 2, 1, 0), lambda m: way, over)
             save(A, B, block, x)
 
 
 def compact_events(A, B):
     lane, sub = lanes(), subs()
-    heads = [pltpu.roll(A[block], 7, 0) for block in (0, 16)]
+    first_edge = (lane & 7) == 0
+    lows, ends, blocks = [], [], []
+    for block in (0, 16):
+        x = load(A, B, block)
+        low = [x[0][1]]
+        for m in range(1, 16):
+            low.append(jnp.where(x[m][0] == x[m - 1][0], jnp.maximum(x[m][1], low[-1]), x[m][1]))
+        blocks.append([w for w, _ in x])
+        lows.append(low)
+        ends.append((pltpu.roll(x[15][0], 1, 0), pltpu.roll(low[15], 1, 0)))
+    beside = [tuple(pltpu.roll(t, 1, 1) for t in e) for e in ends]
+    across = [beside[1], tuple(pltpu.roll(t, 121, 1) for t in ends[0])]
+    flag = jnp.zeros((8, 128), jnp.int32)
+    for h in range(2):
+        w_before, k_before = (
+            jnp.where(sub == 0, jnp.where(first_edge, far, near), own) for far, near, own in zip(across[h], beside[h], ends[h])
+        )
+        w = blocks[h]
+        goes_on = w[0] == w_before
+        flag = flag | (goes_on & (w[0] == w[15])).astype(jnp.int32)
+        carry = jnp.where(goes_on, k_before, 0)
+        lows[h] = [jnp.where(w[m] == w[0], jnp.maximum(lows[h][m], carry), lows[h][m]) for m in range(16)]
+    cells = [[((w ^ SIGN) >> 13) & 0x7FFFF for w in blocks[h]] for h in range(2)]
+    heads = [pltpu.roll(cells[h][0], 7, 0) for h in range(2)]
     nexts = [pltpu.roll(x, 127, 1) for x in heads]
     edge = (lane & 7) == 7
     follows = [
@@ -280,17 +313,18 @@
         jnp.where(sub == 7, jnp.where(edge, nexts[0], nexts[1]), heads[1]),
     ]
     sums = []
-    for block in (0, 16):
+    for h in range(2):
         run = jnp.zeros((8, 128), jnp.int32)
+        x = []
         for m in range(16):
-            c = A[block + m]
-            keep = c != (A[block + m + 1] if m < 15 else follows[block // 16])
-            if block + m == 31:
+            c = cells[h][m]
+            keep = c != (cells[h][m + 1] if m < 15 else follows[h])
+            if h * 16 + m == 31:
                 keep = keep | ((sub == 7) & (lane == 127))
-            w = (run << 16) | (c & 0xFFFF)
-            B[block + m] = B[block + m] | ((c >> 16) << 27)
-            A[block + m] = jnp.where(keep, SIGN | w, 0)
+            key = ((blocks[h][m] & 0x1FFF) << 14) | lows[h][m] | ((c >> 16) << 27)
+            x.append((jnp.where(keep, SIGN | (run << 16) | (c & 0xFFFF), 0), key))
             run = run + keep.astype(jnp.int32)
+        save(A, B, 16 * h, x)
         sums.append(sub_prefix(run))
     orders = [lambda l: ((l >> 3) << 4) + (l & 7), lambda l: ((l >> 3) << 4) + (l & 7) + 8]
     parts = [lane_prefix(sums[h][1], orders[h], orders) for h in range(2)]
@@ -314,7 +348,7 @@
         move_v(x, [(11 + i, i) for i in range(4)])
         y += x[:8]
     starts = group_starts([k >> 27 for _, k in y], [w < 0 for w, _ in y])
-    flag = crowded(starts, CAP) | (every > 8 * CAP).astype(jnp.int32)
+    flag = flag | crowded(starts, CAP) | (every > 8 * CAP).astype(jnp.int32)
     y = aimed([(w, k & 0x7FFFFFF) for w, k in y], [k >> 27 for _, k in y], [w < 0 for w, _ in y], starts, 0xFFFF)
     return y, flag
 
@@ -464,14 +498,14 @@
     return made
 
 
-def spread_lists(inbox, s):
+def spread_lists(inbox, pair):
     x = []
     mask = SIGN | np.int32(3 << 27)
-    for t in (s, s + 1):
-        pair = short_list(inbox, t)
+    for s in pair:
+        words = short_list(inbox, s)
         for high in range(4):
             mine = SIGN | np.int32(high << 27)
-            some = [(jnp.where((w & mask) == mine, w, 0), k) for w, k in pair]
+            some = [(jnp.where((w & mask) == mine, w, 0), k) for w, k in words]
             move_v(some, [(10, 0)])
             x += some
     move_s(x, [(9, 2), (8, 1), (7, 0)])
@@ -516,7 +550,7 @@
                 device_id=peer(phase, j),
                 device_id_type=MESH,
             )
-            for j in range(1, 8)
+            for j in FAR_FIRST[phase]
         ]
 
     sort_events(cell, vehicle, speed, A, B)
@@ -550,11 +584,11 @@
     for c in flags2:
         c.start()
     tables = []
-    for s in range(0, 8, 2):
-        for j in (s, s + 1):
+    for pair in ((0, 1), (2, 6), (3, 7), (4, 5)):
+        for j in pair:
             if j:
-                second[j - 1].wait_recv()
-        tables.append(spread_lists(in2, s))
+                second[FAR_FIRST[1].index(j)].wait_recv()
+        tables.append(spread_lists(in2, pair))
     table = joined(tables)
     for c in flags2:
         c.wait_recv()

time: 40.5 us -> 39.2 us (0.968)
  Pallas kernels: 38.2 us -> 36.9 us
    pallas_call x1, Pallas kernels: 38.2 us -> 36.9 us  [sparse_path(): pl.pallas_call(exchange_kernel, out_shape=(jax.ShapeDtypeStruct((2, 8, 12...]
where the time goes in v2:
time: 39.2 us; the launch traced here: 39 us
  Pallas kernels  36.9 us (94%)
  between operations  1.32 us (3%)
  other arithmetic  0.6 us (2%)
    pallas_call x1, Pallas kernels, sparse_path(): pl.pallas_call(exchange_kernel, out_shape=(jax.ShapeDtypeStruct((2, 8, 12...  36.9 us

profile of v2, /device:TPU:1, one launch (start us, length us, event | category | flops | bytes accessed | tf_op | source)
XLA Modules:
  0.0 39.0 jit_solution(7297653191260439919)
XLA Ops:
  0.6 36.9 %shard_map.50 = (f32[2,8,128]{2,1,0:T(8,128)S(1)}, s32[1,1]{1,0:T(1,128)}) custom-call(s32[32,8,128]{2,1,0:T(8,128)} %bitcast.14, s32[32,8,128]{2,1,0:T(8,128)} %bitcast.15, f32[32,8,128]{2,1,0:T(8,128)} %bitcast.16), custom_call_target="tpu_custom_call" | custom-call | tf_op jit(solution)/shard_map/pallas_call | solution.py:627
  38.2 0.2 conditional.1
  38.4 0.6 %fusion.23 = (s32[1024]{0:T(1024)}, f32[1024]{0:T(1024)}) fusion(f32[2,8,128]{2,1,0:T(8,128)S(1)} %get-tuple-element.57), kind=kLoop, calls=%fused_computation.95 | loop fusion | flops 1024 | bytes 16384 | tf_op jit(solution)/shard_map/convert_element_type | solution.py:650

commit v3 on v2

--- a/solution.py
+++ b/solution.py
@@ -312,7 +312,7 @@
         jnp.where(sub == 7, jnp.where(edge, pltpu.roll(heads[1], 7, 1), nexts[0]), heads[0]),
         jnp.where(sub == 7, jnp.where(edge, nexts[0], nexts[1]), heads[1]),
     ]
-    sums = []
+    sums, keeps = [], []
     for h in range(2):
         run = jnp.zeros((8, 128), jnp.int32)
         x = []
@@ -321,6 +321,7 @@
             keep = c != (cells[h][m + 1] if m < 15 else follows[h])
             if h * 16 + m == 31:
                 keep = keep | ((sub == 7) & (lane == 127))
+            keeps.append(keep)
             key = ((blocks[h][m] & 0x1FFF) << 14) | lows[h][m] | ((c >> 16) << 27)
             x.append((jnp.where(keep, SIGN | (run << 16) | (c & 0xFFFF), 0), key))
             run = run + keep.astype(jnp.int32)
@@ -329,9 +330,10 @@
     orders = [lambda l: ((l >> 3) << 4) + (l & 7), lambda l: ((l >> 3) << 4) + (l & 7) + 8]
     parts = [lane_prefix(sums[h][1], orders[h], orders) for h in range(2)]
     every = parts[0][2] + parts[1][2]
+    starts = group_starts(cells[0] + cells[1], keeps, every, 16)
     for h in range(2):
-        start = (parts[0][h] + parts[1][h] + sums[h][0]) << 16
-        x = [(jnp.where(w < 0, w + start, 0), k) for w, k in load(A, B, 16 * h)]
+        ahead = (parts[0][h] + parts[1][h] + sums[h][0]) << 16
+        x = [(jnp.where(w < 0, w + ahead, 0), k) for w, k in load(A, B, 16 * h)]
         move_v(x, [(i, i) for i in range(4)])
         move_s(x, [(4 + i, i) for i in range(3)])
         x = turned(x)
@@ -347,7 +349,6 @@
         x = load(A, B, 16 * h)
         move_v(x, [(11 + i, i) for i in range(4)])
         y += x[:8]
-    starts = group_starts([k >> 27 for _, k in y], [w < 0 for w, _ in y])
     flag = flag | crowded(starts, CAP) | (every > 8 * CAP).astype(jnp.int32)
     y = aimed([(w, k & 0x7FFFFFF) for w, k in y], [k >> 27 for _, k in y], [w < 0 for w, _ in y], starts, 0xFFFF)
     return y, flag
@@ -358,15 +359,15 @@
     return (v & 7) * CAP + ((v >> 3) << 10) + (subs() << 7) + ((lane & 7) << 4) + (lane >> 3)
 
 
-def group_starts(groups, valid):
-    groups = [jnp.where(u, g, 8) for g, u in zip(groups, valid)]
+def group_starts(cells, keeps, every, shift):
+    cells = [jnp.where(u, c, CELLS) for c, u in zip(cells, keeps)]
     starts = [jnp.zeros((8, 128), jnp.int32)]
-    for j in range(1, 9):
+    for j in range(1, 8):
         t = jnp.zeros((8, 128), jnp.int32)
-        for g in groups:
-            t = t + jnp.where(g < j, 1, 0)
+        for c in cells:
+            t = t + jnp.where(c < j << shift, 1, 0)
         starts.append(total(t))
-    return starts
+    return starts + [every]
 
 
 def crowded(starts, room):
@@ -447,25 +448,28 @@
     return x
 
 
-def best_of_cells(x):
+def best_of_cells(x, tell):
     lane, sub = lanes(), subs()
     head = pltpu.roll(x[0][0], 7, 0)
     beyond = jnp.where(lane < 64, pltpu.roll(head, 71, 1), pltpu.roll(head, 63, 1))
     carried = jnp.where((lane & 7) == 7, beyond, pltpu.roll(head, 127, 1))
     follow = jnp.where(sub == 7, carried, head)
     run = jnp.zeros((8, 128), jnp.int32)
-    y = []
+    y, keeps = [], []
     for m in range(16):
         c, k = x[m]
         keep = c != (x[m + 1][0] if m < 15 else follow)
         if m == 15:
             keep = keep | ((sub == 7) & (lane == 127))
         keep = keep & (c < EMPTY)
+        keeps.append(keep)
         y.append((jnp.where(keep, SIGN | (run << 16) | c, 0), k))
         run = run + keep.astype(jnp.int32)
     within, block = sub_prefix(run)
     order = lambda l: (((l >> 3) & 7) << 4) + ((l >> 6) << 3) + (l & 7)
-    ahead = lane_prefix(block, order, [order])[0]
+    ahead, every = lane_prefix(block, order, [order])
+    starts = group_starts([c for c, _ in x], keeps, every, 13)
+    tell(crowded(starts, SHORT))
     start = (within + ahead) << 16
     y = [(jnp.where(w < 0, w + start, 0), k) for w, k in y]
     move_v(y, [(i, i) for i in range(4)])
@@ -473,15 +477,14 @@
     y = turned(y)
     move_s(y, [(7 + i, i) for i in range(3)])
     move_v(y, [(10, 3), (11, 0), (12, 1), (13, 2)])
-    return y
-
-
-def regroup(x):
-    y = best_of_cells(x)
+    return y, starts
+
+
+def regroup(x, tell):
+    y, starts = best_of_cells(x, tell)
     groups = [(w >> 13) & 7 for w, _ in y]
     valid = [w < 0 for w, _ in y]
-    starts = group_starts(groups, valid)
-    return expand_lists(aimed(y, groups, valid, starts, 0x1FFF)), crowded(starts, SHORT)
+    return expand_lists(aimed(y, groups, valid, starts, 0x1FFF))
 
 
 def short_list(inbox, s):
@@ -523,10 +526,17 @@
     return [jnp.maximum(t[8 * z : 8 * z + 8], t[64 + 8 * z : 72 + 8 * z]) for z in range(8)]
 
 
-def exchange_kernel(cell, vehicle, speed, both, flags, A, B, out1, in1, out2, in2, out3, in3, mark, marks1, mark2,
-                    marks2, send, recv):
+def exchange_kernel(cell, vehicle, speed, both, flags, events, reals, A, B, out1, in1, out2, in2, out3, in3, mark, marks,
+                    arrive, send, recv):
     gx, gy = lax.axis_index("gx"), lax.axis_index("gy")
     y, z = gy // 8, gy % 8
+    loads = [
+        pltpu.make_async_copy(cell, events.at[0], arrive.at[0]),
+        pltpu.make_async_copy(vehicle, events.at[1], arrive.at[1]),
+        pltpu.make_async_copy(speed, reals, arrive.at[2]),
+    ]
+    for c in loads:
+        c.start()
 
     def peer(phase, j):
         if phase == 0:
@@ -544,7 +554,7 @@
         return [
             pltpu.make_async_remote_copy(
                 src_ref=source(j),
-                dst_ref=target.at[j],
+                dst_ref=target(j),
                 send_sem=send.at[row, j],
                 recv_sem=recv.at[row, j],
                 device_id=peer(phase, j),
@@ -553,66 +563,72 @@
             for j in FAR_FIRST[phase]
         ]
 
-    sort_events(cell, vehicle, speed, A, B)
+    def share(phase, seen):
+        mark[phase] = seen
+        made = copies(3 + phase, phase, lambda j: mark.at[phase], lambda j: marks.at[phase, j])
+        for c in made:
+            c.start()
+        return made
+
+    def seen_by(phase, made, seen):
+        for c in made:
+            c.wait_recv()
+        for j in range(1, 8):
+            seen = jnp.maximum(seen, marks[phase, j])
+        return seen
+
+    for c in loads:
+        c.wait()
+    sort_events(events.at[0], events.at[1], reals, A, B)
     x, flag = compact_events(A, B)
     pack_messages(expand_lists(x), out1)
     pl.semaphore_wait(barrier, 21)
-    first = copies(0, 0, lambda j: out1.at[gx ^ j], in1)
+    first = copies(0, 0, lambda j: out1.at[gx ^ j], lambda j: in1.at[j])
     for c in first:
         c.start()
     in1[0] = out1[gx]
     for c in first:
         c.wait_recv()
 
-    x, more = regroup(merge_lists(in1))
-    mark[...] = (flag | more).astype(jnp.float32)
+    told = []
+
+    def tell(more):
+        seen = jnp.max((flag | more).astype(jnp.float32), axis=0, keepdims=True)
+        told.append((share(0, seen), seen))
+
+    x = regroup(merge_lists(in1), tell)
     pack_short(x, out2)
-    second = copies(1, 1, lambda j: out2.at[y ^ j], in2)
+    second = copies(1, 1, lambda j: out2.at[y ^ j], lambda j: in2.at[j])
     for c in second:
         c.start()
-    flags1 = copies(2, 0, lambda j: mark, marks1)
-    for c in flags1:
-        c.start()
     in2[0] = out2[y]
-    for c in flags1:
-        c.wait_recv()
-    seen = mark[...]
-    for j in range(1, 8):
-        seen = jnp.maximum(seen, marks1[j])
-    mark2[...] = seen
-    flags2 = copies(3, 1, lambda j: mark2, marks2)
-    for c in flags2:
-        c.start()
+    seen = seen_by(0, *told[0])
+    told.append((share(2, seen), seen))
+
     tables = []
     for pair in ((0, 1), (2, 6), (3, 7), (4, 5)):
         for j in pair:
             if j:
                 second[FAR_FIRST[1].index(j)].wait_recv()
         tables.append(spread_lists(in2, pair))
-    table = joined(tables)
-    for c in flags2:
-        c.wait_recv()
-    for j in range(1, 8):
-        seen = jnp.maximum(seen, marks2[j])
-    for v, k in enumerate(table):
+    for v, k in enumerate(joined(tables)):
         there = k >= 0
         out3[v, 0] = jnp.where(there, (k >> 10).astype(jnp.float32) * (1.0 / 1024.0), -1.0)
-        out3[v, 1] = jnp.where(there, (1023 - (k & 1023)).astype(jnp.float32), 1024.0) + seen * 4096.0
-    third = copies(4, 2, lambda j: out3.at[z ^ j], in3)
+        out3[v, 1] = jnp.where(there, (1023 - (k & 1023)).astype(jnp.float32), 1024.0)
+    third = copies(2, 2, lambda j: out3.at[z ^ j], lambda j: in3.at[j])
     for c in third:
         c.start()
+    seen = seen_by(2, *told[1])
+    told.append((share(1, seen), seen))
     in3[0] = out3[z]
-    for c in third:
-        c.wait_recv()
     k = key_of(in3[0, 0], in3[0, 1])
-    most = in3[0, 1]
-    for j in range(1, 8):
+    for j in reversed(FAR_FIRST[2]):
+        third[FAR_FIRST[2].index(j)].wait_recv()
         k = jnp.maximum(k, key_of(in3[j, 0], in3[j, 1]))
-        most = jnp.maximum(most, in3[j, 1])
     both[0] = jnp.where(k < 0, -1.0, (k >> 10).astype(jnp.float32) * (1.0 / 1024.0))
     both[1] = jnp.where(k < 0, -1, 1023 - (k & 1023)).astype(jnp.float32)
-    flags[0, 0] = jnp.max(most).astype(jnp.int32)
-    for group in (first, second, flags1, flags2, third):
+    flags[0, 0] = jnp.max(seen_by(1, *told[2])).astype(jnp.int32)
+    for group in (first, second, third, *(made for made, _ in told)):
         for c in group:
             c.wait_send()
 
@@ -630,14 +646,24 @@
             jax.ShapeDtypeStruct((2, 8, 128), jnp.float32),
             jax.ShapeDtypeStruct((1, 1), jnp.int32),
         ),
-        in_specs=[whole] * 3,
+        in_specs=[pl.BlockSpec(memory_space=pl.ANY)] * 3,
         out_specs=(whole, pl.BlockSpec(memory_space=pltpu.SMEM)),
         scratch_shapes=[
-            ints(32), ints(32),
-            words(8, 6), words(8, 6), pltpu.VMEM((8, 9, 4, 128), jnp.float32), pltpu.VMEM((8, 9, 4, 128), jnp.float32), words(8, 2), words(8, 2),
-            words(), words(8), words(), words(8),
-            pltpu.SemaphoreType.DMA((5, 8)),
-            pltpu.SemaphoreType.DMA((5, 8)),
+            pltpu.VMEM((2, 32, 8, 128), jnp.int32),
+            words(32),
+            ints(32),
+            ints(32),
+            words(8, 6),
+            words(8, 6),
+            pltpu.VMEM((8, 9, 4, 128), jnp.float32),
+            pltpu.VMEM((8, 9, 4, 128), jnp.float32),
+            words(8, 2),
+            words(8, 2),
+            pltpu.VMEM((3, 1, 128), jnp.float32),
+            pltpu.VMEM((3, 8, 1, 128), jnp.float32),
+            pltpu.SemaphoreType.DMA((3,)),
+            pltpu.SemaphoreType.DMA((6, 8)),
+            pltpu.SemaphoreType.DMA((6, 8)),
         ],
         compiler_params=pltpu.CompilerParams(collective_id=0, has_side_effects=True),
     )(cell, vehicle, speed)
@@ -646,7 +672,7 @@
 def per_device(cell, vehicle, speed):
     shaped = [x.reshape(32, 8, 128) for x in (cell, vehicle, speed)]
     both, flags = sparse_path(*shaped)
-    both = lax.cond(flags[0, 0] > 2048, lambda: dense_path(cell, vehicle, speed), lambda: both)
+    both = lax.cond(flags[0, 0] > 0, lambda: dense_path(cell, vehicle, speed), lambda: both)
     return both[0].reshape(1024), both[1].astype(jnp.int32).reshape(1024)
 
 

time: 39.2 us -> 37.8 us (0.964)
  Pallas kernels: 36.9 us -> 35.5 us
    pallas_call x1, Pallas kernels: 36.9 us -> 35.5 us  [sparse_path(): pl.pallas_call(exchange_kernel, out_shape=(jax.ShapeDtypeStruct((2, 8, 12...]
where the time goes in v3:
time: 37.8 us; the launch traced here: 37.6 us
  Pallas kernels  35.5 us (94%)
  between operations  1.32 us (3%)
  other arithmetic  0.6 us (2%)
    pallas_call x1, Pallas kernels, sparse_path(): pl.pallas_call(exchange_kernel, out_shape=(jax.ShapeDtypeStruct((2, 8, 12...  35.5 us

profile of v3, /device:TPU:1, one launch (start us, length us, event | category | flops | bytes accessed | tf_op | source)
XLA Modules:
  0.0 37.6 jit_solution(974052415149338172)
XLA Ops:
  0.6 35.5 %shard_map.50 = (f32[2,8,128]{2,1,0:T(8,128)S(1)}, s32[1,1]{1,0:T(1,128)}) custom-call(s32[32,8,128]{2,1,0:T(8,128)} %bitcast.14, s32[32,8,128]{2,1,0:T(8,128)} %bitcast.15, f32[32,8,128]{2,1,0:T(8,128)} %bitcast.16), custom_call_target="tpu_custom_call" | custom-call | tf_op jit(solution)/shard_map/pallas_call | solution.py:643
  36.8 0.2 conditional.1
  37.0 0.6 %fusion.23 = (s32[1024]{0:T(1024)}, f32[1024]{0:T(1024)}) fusion(f32[2,8,128]{2,1,0:T(8,128)S(1)} %get-tuple-element.57), kind=kLoop, calls=%fused_computation.95 | loop fusion | flops 1024 | bytes 16384 | tf_op jit(solution)/shard_map/convert_element_type | solution.py:676

commit v4 on v3

--- a/solution.py
+++ b/solution.py
@@ -526,8 +526,8 @@
     return [jnp.maximum(t[8 * z : 8 * z + 8], t[64 + 8 * z : 72 + 8 * z]) for z in range(8)]
 
 
-def exchange_kernel(cell, vehicle, speed, both, flags, events, reals, A, B, out1, in1, out2, in2, out3, in3, mark, marks,
-                    arrive, send, recv):
+def exchange_kernel(cell, vehicle, speed, both, flags, events, reals, A, B, out1, in1, out2, in2, out3, in3, mark, plane,
+                    marks, arrive, send, recv, plane_send, plane_recv):
     gx, gy = lax.axis_index("gx"), lax.axis_index("gy")
     y, z = gy // 8, gy % 8
     loads = [
@@ -545,10 +545,18 @@
             return (gx, (y ^ j) * 8 + z)
         return (gx, y * 8 + (z ^ j))
 
+    def in_plane(j):
+        return (gx ^ (j & 7), y * 8 + (z ^ (j >> 3)))
+
     barrier = pltpu.get_barrier_semaphore()
-    for phase in range(3):
-        for j in range(1, 8):
-            pl.semaphore_signal(barrier, inc=1, device_id=peer(phase, j), device_id_type=MESH)
+    for j in range(1, 8):
+        pl.semaphore_signal(barrier, inc=1, device_id=peer(1, j), device_id_type=MESH)
+
+    def greet(j, _):
+        pl.semaphore_signal(barrier, inc=1, device_id=in_plane(j), device_id_type=MESH)
+        return 0
+
+    lax.fori_loop(1, 64, greet, 0)
 
     def copies(row, phase, source, target):
         return [
@@ -563,26 +571,29 @@
             for j in FAR_FIRST[phase]
         ]
 
-    def share(phase, seen):
-        mark[phase] = seen
-        made = copies(3 + phase, phase, lambda j: mark.at[phase], lambda j: marks.at[phase, j])
-        for c in made:
-            c.start()
-        return made
-
-    def seen_by(phase, made, seen):
-        for c in made:
-            c.wait_recv()
-        for j in range(1, 8):
-            seen = jnp.maximum(seen, marks[phase, j])
-        return seen
+    def to_plane(j):
+        return pltpu.make_async_remote_copy(
+            src_ref=plane.at[0],
+            dst_ref=plane.at[j],
+            send_sem=plane_send.at[j],
+            recv_sem=plane_recv.at[j],
+            device_id=in_plane(j),
+            device_id_type=MESH,
+        )
+
+    def over_plane(act):
+        def step(j, _):
+            act(to_plane(j))
+            return 0
+
+        lax.fori_loop(1, 64, step, 0)
 
     for c in loads:
         c.wait()
     sort_events(events.at[0], events.at[1], reals, A, B)
     x, flag = compact_events(A, B)
     pack_messages(expand_lists(x), out1)
-    pl.semaphore_wait(barrier, 21)
+    pl.semaphore_wait(barrier, 70)
     first = copies(0, 0, lambda j: out1.at[gx ^ j], lambda j: in1.at[j])
     for c in first:
         c.start()
@@ -590,11 +601,8 @@
     for c in first:
         c.wait_recv()
 
-    told = []
-
     def tell(more):
-        seen = jnp.max((flag | more).astype(jnp.float32), axis=0, keepdims=True)
-        told.append((share(0, seen), seen))
+        plane[0] = jnp.max((flag | more).astype(jnp.float32), axis=0, keepdims=True)
 
     x = regroup(merge_lists(in1), tell)
     pack_short(x, out2)
@@ -602,8 +610,7 @@
     for c in second:
         c.start()
     in2[0] = out2[y]
-    seen = seen_by(0, *told[0])
-    told.append((share(2, seen), seen))
+    over_plane(lambda c: c.start())
 
     tables = []
     for pair in ((0, 1), (2, 6), (3, 7), (4, 5)):
@@ -618,19 +625,28 @@
     third = copies(2, 2, lambda j: out3.at[z ^ j], lambda j: in3.at[j])
     for c in third:
         c.start()
-    seen = seen_by(2, *told[1])
-    told.append((share(1, seen), seen))
     in3[0] = out3[z]
+    over_plane(lambda c: c.wait_recv())
+    mark[...] = jnp.max(plane[...], axis=0)
+    told = copies(3, 1, lambda j: mark, lambda j: marks.at[j])
+    for c in told:
+        c.start()
     k = key_of(in3[0, 0], in3[0, 1])
     for j in reversed(FAR_FIRST[2]):
         third[FAR_FIRST[2].index(j)].wait_recv()
         k = jnp.maximum(k, key_of(in3[j, 0], in3[j, 1]))
     both[0] = jnp.where(k < 0, -1.0, (k >> 10).astype(jnp.float32) * (1.0 / 1024.0))
     both[1] = jnp.where(k < 0, -1, 1023 - (k & 1023)).astype(jnp.float32)
-    flags[0, 0] = jnp.max(seen_by(1, *told[2])).astype(jnp.int32)
-    for group in (first, second, third, *(made for made, _ in told)):
+    seen = mark[...]
+    for c in told:
+        c.wait_recv()
+    for j in range(1, 8):
+        seen = jnp.maximum(seen, marks[j])
+    flags[0, 0] = jnp.max(seen).astype(jnp.int32)
+    for group in (first, second, third, told):
         for c in group:
             c.wait_send()
+    over_plane(lambda c: c.wait_send())
 
 
 def words(*shape):
@@ -659,11 +675,14 @@
             pltpu.VMEM((8, 9, 4, 128), jnp.float32),
             words(8, 2),
             words(8, 2),
-            pltpu.VMEM((3, 1, 128), jnp.float32),
-            pltpu.VMEM((3, 8, 1, 128), jnp.float32),
+            pltpu.VMEM((1, 128), jnp.float32),
+            pltpu.VMEM((64, 1, 128), jnp.float32),
+            pltpu.VMEM((8, 1, 128), jnp.float32),
             pltpu.SemaphoreType.DMA((3,)),
-            pltpu.SemaphoreType.DMA((6, 8)),
-            pltpu.SemaphoreType.DMA((6, 8)),
+            pltpu.SemaphoreType.DMA((4, 8)),
+            pltpu.SemaphoreType.DMA((4, 8)),
+            pltpu.SemaphoreType.DMA((64,)),
+            pltpu.SemaphoreType.DMA((64,)),
         ],
         compiler_params=pltpu.CompilerParams(collective_id=0, has_side_effects=True),
     )(cell, vehicle, speed)

time: 37.8 us -> 38.6 us (1.021)
  Pallas kernels: 35.5 us -> 36.1 us
    pallas_call x1, Pallas kernels: 35.5 us -> 36.1 us  [sparse_path(): pl.pallas_call(exchange_kernel, out_shape=(jax.ShapeDtypeStruct((2, 8, 12...]
where the time goes in v4:
time: 38.6 us; the launch traced here: 38.2 us
  Pallas kernels  36.1 us (94%)
  between operations  1.32 us (3%)
  other arithmetic  0.6 us (2%)
    pallas_call x1, Pallas kernels, sparse_path(): pl.pallas_call(exchange_kernel, out_shape=(jax.ShapeDtypeStruct((2, 8, 12...  36.1 us

profile of v4, /device:TPU:1, one launch (start us, length us, event | category | flops | bytes accessed | tf_op | source)
XLA Modules:
  0.0 38.2 jit_solution(17295956559973254006)
XLA Ops:
  0.6 36.1 %shard_map.50 = (f32[2,8,128]{2,1,0:T(8,128)S(1)}, s32[1,1]{1,0:T(1,128)}) custom-call(s32[32,8,128]{2,1,0:T(8,128)} %bitcast.14, s32[32,8,128]{2,1,0:T(8,128)} %bitcast.15, f32[32,8,128]{2,1,0:T(8,128)} %bitcast.16), custom_call_target="tpu_custom_call" | custom-call | tf_op jit(solution)/shard_map/pallas_call | solution.py:659
  37.4 0.2 conditional.1
  37.6 0.6 %fusion.23 = (s32[1024]{0:T(1024)}, f32[1024]{0:T(1024)}) fusion(f32[2,8,128]{2,1,0:T(8,128)S(1)} %get-tuple-element.57), kind=kLoop, calls=%fused_computation.95 | loop fusion | flops 1024 | bytes 16384 | tf_op jit(solution)/shard_map/convert_element_type | solution.py:695

commit v5 on v3

--- a/solution.py
+++ b/solution.py
@@ -280,7 +280,7 @@
             save(A, B, block, x)
 
 
-def compact_events(A, B):
+def compact_events(A, B, me):
     lane, sub = lanes(), subs()
     first_edge = (lane & 7) == 0
     lows, ends, blocks = [], [], []
@@ -350,7 +350,7 @@
         move_v(x, [(11 + i, i) for i in range(4)])
         y += x[:8]
     flag = flag | crowded(starts, CAP) | (every > 8 * CAP).astype(jnp.int32)
-    y = aimed([(w, k & 0x7FFFFFF) for w, k in y], [k >> 27 for _, k in y], [w < 0 for w, _ in y], starts, 0xFFFF)
+    y = aimed([(w, k & 0x7FFFFFF) for w, k in y], [k >> 27 for _, k in y], [w < 0 for w, _ in y], starts, 0xFFFF, me)
     return y, flag
 
 
@@ -377,14 +377,17 @@
     return (most > room).astype(jnp.int32)
 
 
-def aimed(x, groups, valid, starts, mask):
+def aimed(x, groups, valid, starts, mask, me=None):
     made = []
     for v, (w, k) in enumerate(x):
         target = list_rank(v)
         moved = jnp.zeros((8, 128), jnp.int32)
         for j in range(1, 8):
             moved = jnp.where(groups[v] == j, j * CAP - starts[j], moved)
-        made.append((jnp.where(valid[v], SIGN | ((target + moved) << 16) | (w & mask), 0), k))
+        target = target + moved
+        if me is not None:
+            target = target ^ (-((groups[v] ^ me) & 1) & (CAP - 1))
+        made.append((jnp.where(valid[v], SIGN | (target << 16) | (w & mask), 0), k))
     return made
 
 
@@ -426,23 +429,15 @@
 
 
 def merge_lists(inbox):
-    around, back = 7 - subs(), 127 - lanes()
-    x = [None] * 16
-    for s in range(8):
-        for h in range(2):
-            pair = (inbox[s, h].astype(jnp.int32), key_of(inbox[s, 2 + h], inbox[s, 4 + h]))
-            if s & 1:
-                x[8 * (1 - h) + s] = tuple(lane_pick(sub_pick(w, around), back) for w in pair)
-            else:
-                x[8 * h + s] = pair
+    x = [(inbox[s, h].astype(jnp.int32), key_of(inbox[s, 2 + h], inbox[s, 4 + h])) for h in range(2) for s in range(8)]
     for level in (1, 2, 3):
         down = (lambda m: bool(m >> level & 1)) if level < 3 else (lambda m: False)
         way = lane_bit(3 + level) if level < 3 else False
-        order_v(x, (*reversed(range(level)), 3), down)
-        order_s(x, (2, 1, 0), down)
+        order_v(x, (*reversed(range(level)), 3), down, over)
+        order_s(x, (2, 1, 0), down, over)
         x = turned(x)
-        order_s(x, (2, 1, 0), lambda m: way)
-        order_v(x, (3, 2, 1, 0), lambda m: way)
+        order_s(x, (2, 1, 0), lambda m: way, over)
+        order_v(x, (3, 2, 1, 0), lambda m: way, over)
         if level < 3:
             x = turned(x)
     return x
@@ -454,10 +449,19 @@
     beyond = jnp.where(lane < 64, pltpu.roll(head, 71, 1), pltpu.roll(head, 63, 1))
     carried = jnp.where((lane & 7) == 7, beyond, pltpu.roll(head, 127, 1))
     follow = jnp.where(sub == 7, carried, head)
+    keys = [x[0][1]]
+    for m in range(1, 16):
+        keys.append(jnp.where(x[m][0] == x[m - 1][0], jnp.maximum(x[m][1], keys[-1]), x[m][1]))
+    before = []
+    for t in (pltpu.roll(x[15][0], 1, 0), pltpu.roll(keys[15], 1, 0)):
+        far = jnp.where(lane < 64, pltpu.roll(t, 65, 1), pltpu.roll(t, 57, 1))
+        before.append(jnp.where(sub == 0, jnp.where((lane & 7) == 0, far, pltpu.roll(t, 1, 1)), t))
+    carry = jnp.where(x[0][0] == before[0], before[1], 0)
     run = jnp.zeros((8, 128), jnp.int32)
     y, keeps = [], []
     for m in range(16):
-        c, k = x[m]
+        c = x[m][0]
+        k = jnp.where(c == x[0][0], jnp.maximum(keys[m], carry), keys[m])
         keep = c != (x[m + 1][0] if m < 15 else follow)
         if m == 15:
             keep = keep | ((sub == 7) & (lane == 127))
@@ -580,7 +584,7 @@
     for c in loads:
         c.wait()
     sort_events(events.at[0], events.at[1], reals, A, B)
-    x, flag = compact_events(A, B)
+    x, flag = compact_events(A, B, gx)
     pack_messages(expand_lists(x), out1)
     pl.semaphore_wait(barrier, 21)
     first = copies(0, 0, lambda j: out1.at[gx ^ j], lambda j: in1.at[j])
@@ -621,6 +625,9 @@
     seen = seen_by(2, *told[1])
     told.append((share(1, seen), seen))
     in3[0] = out3[z]
+    for group in (first, second, told[0][0], told[1][0]):
+        for c in group:
+            c.wait_send()
     k = key_of(in3[0, 0], in3[0, 1])
     for j in reversed(FAR_FIRST[2]):
         third[FAR_FIRST[2].index(j)].wait_recv()
@@ -628,7 +635,7 @@
     both[0] = jnp.where(k < 0, -1.0, (k >> 10).astype(jnp.float32) * (1.0 / 1024.0))
     both[1] = jnp.where(k < 0, -1, 1023 - (k & 1023)).astype(jnp.float32)
     flags[0, 0] = jnp.max(seen_by(1, *told[2])).astype(jnp.int32)
-    for group in (first, second, third, *(made for made, _ in told)):
+    for group in (third, told[2][0]):
         for c in group:
             c.wait_send()
 

time: 37.8 us -> 37.8 us (level)
  no operation moved by 1% of the time
where the time goes in v5:
time: 37.8 us; the launch traced here: 37.7 us
  Pallas kernels  35.6 us (94%)
  between operations  1.32 us (3%)
  other arithmetic  0.6 us (2%)
    pallas_call x1, Pallas kernels, sparse_path(): pl.pallas_call(exchange_kernel, out_shape=(jax.ShapeDtypeStruct((2, 8, 12...  35.6 us

profile of v5, /device:TPU:1, one launch (start us, length us, event | category | flops | bytes accessed | tf_op | source)
XLA Modules:
  0.0 37.7 jit_solution(11565403454375717725)
XLA Ops:
  0.6 35.6 %shard_map.50 = (f32[2,8,128]{2,1,0:T(8,128)S(1)}, s32[1,1]{1,0:T(1,128)}) custom-call(s32[32,8,128]{2,1,0:T(8,128)} %bitcast.14, s32[32,8,128]{2,1,0:T(8,128)} %bitcast.15, f32[32,8,128]{2,1,0:T(8,128)} %bitcast.16), custom_call_target="tpu_custom_call" | custom-call | tf_op jit(solution)/shard_map/pallas_call | solution.py:650
  36.9 0.2 conditional.1
  37.1 0.6 %fusion.23 = (s32[1024]{0:T(1024)}, f32[1024]{0:T(1024)}) fusion(f32[2,8,128]{2,1,0:T(8,128)S(1)} %get-tuple-element.57), kind=kLoop, calls=%fused_computation.95 | loop fusion | flops 1024 | bytes 16384 | tf_op jit(solution)/shard_map/convert_element_type | solution.py:683
